TPU v7x, 256 devices: a 2x2x32 block of a 4x8x32 slice. The times are simulated.
256 devices in a mesh: groups: 4 (over x, y), tp: 64 (over z, core).
Axes of the slice: x: 2, y: 2, z: 32, core: 2. Of those that a mesh axis runs over, the one named last changes fastest.
The devices are a block of a 4x8x32 slice.
Arguments:
- queries: bfloat16 [8, 4096, 4096], P('groups', 'tp'), parts along dimension 0, may hold values from -162 to 162
- keys: bfloat16 [8, 4096, 2048], P('groups', 'tp'), parts along dimension 0, may hold values from -6 to 6
- values: bfloat16 [8, 4096, 2048], P('groups', 'tp'), parts along dimension 0, may hold values from -6 to 6
- lengths: int32 [8], P('groups'), parts along dimension 0, may hold values from 1024 to 4096
Outputs:
- attended: bfloat16 [8, 4096, 4096], P('groups', 'tp'), parts along dimension 0
There are 4 independent parts, one for each index of `groups`. A program takes and returns all parts, laid end to end along the dimension named above; each array names one. Nothing has to cross between parts.
All inputs are finite; a program needn't handle non-finite values.
Results may differ from a plain program's by a relative error of at most 0.0085.
Values may be sent and summed in bfloat16 or wider, within the bound.
No kernel may reach another device: no remote copies, remote signals or barrier semaphores. Data moves between devices by JAX's collectives and lax.ppermute only.
A program may use at most 64 MiB of HBM per device.

v0:
```python
import jax
import jax.numpy as jnp
from jax import lax
from jax.sharding import Mesh
from jax.sharding import PartitionSpec as P

HEADS = 32
KVH = 16
HD = 128
TP = ("tp_0", "tp_1")


query_scale = 144.0 ** (-0.5)
soft_cap = 50.0


def sent_together(arrays, axis, split_dim, concat_dim, along):
    both = jnp.concatenate(arrays, axis=along)
    result, at, finished = (
        lax.all_to_all(both, axis, split_axis=split_dim, concat_axis=concat_dim, tiled=True),
        0,
        [],
    )
    for a in arrays:
        finished.append(lax.slice_in_dim(result, at, at + a.shape[along], axis=along))
        at += a.shape[along]
    return tuple(finished)


def partner(value, axis, apart):
    return lax.ppermute(value, axis, [(i, i ^ 1 << apart) for i in range(lax.axis_size(axis))])


def in_blocks(value, dim, length):
    lengths = value.shape
    parts = value.reshape(*lengths[:dim], length, lengths[dim] // length, *lengths[dim + 1 :])
    return jnp.moveaxis(parts, dim, 0)


def joined_along(parts, dim):
    lengths = list(parts.shape[1:])
    lengths[dim] *= parts.shape[0]
    return jnp.moveaxis(parts, 0, dim).reshape(lengths)


def moved_by_axis(parts, axes, turns):
    inside = parts.shape[1:]
    result = parts.reshape(*(lax.axis_size(a) for a in axes), *inside)
    for k in turns:
        result = lax.all_to_all(result, axes[k], k, k, tiled=True)
    return result.reshape(-1, *inside)


def core_and_chips(value, groups, turns, split_dim, concat_dim):
    length = lax.axis_size(groups[0]) * lax.axis_size(groups[1])
    parts = in_blocks(value, split_dim, length)
    return joined_along(moved_by_axis(parts, groups, turns), concat_dim)


def block_attend(block_q, start, key_rows, value_rows, valid):
    width = block_q.shape[1]
    count = key_rows.shape[1]
    score = (
        jnp.einsum("gqd,gkd->gqk", block_q, key_rows, preferred_element_type=jnp.float32)
        * query_scale
    )
    capped = soft_cap * jnp.tanh(score / soft_cap)
    query_pos = start + jnp.arange(width)
    key_pos = jnp.arange(count)
    allowed = (key_pos[None, None, :] <= query_pos[None, :, None]) & (
        key_pos[None, None, :] < valid[:, None, None]
    )
    weight = jnp.where(allowed, jnp.exp(capped), 0.0)
    total = jnp.sum(weight, axis=2)
    mixed = jnp.einsum(
        "gqk,gkd->gqd", weight.astype(jnp.bfloat16), value_rows, preferred_element_type=jnp.float32
    )
    mixed = mixed / total[:, :, None]
    live = query_pos[None, :] < valid[:, None]
    return jnp.where(live[:, :, None], mixed, 0.0).astype(jnp.bfloat16)


def attend_all(local_q, local_k, local_v, valid):
    items, length, depth = local_q.shape
    width = min(512, length)
    blocks = length // width
    pieces = []
    for index in range(blocks):
        block_q = local_q[:, index * width : (index + 1) * width]
        upper = (index + 1) * width
        pieces.append(
            block_attend(block_q, index * width, local_k[:, :upper], local_v[:, :upper], valid)
        )
    return jnp.concatenate(pieces, axis=1)


def per_device(queries, keys, values, lengths):
    seqs, rows, _ = queries.shape
    devices = lax.axis_size(TP)
    pairs = seqs * HEADS
    owned = pairs // devices
    heads_q = queries.reshape(seqs, rows, HEADS, HD).transpose(0, 2, 1, 3).reshape(pairs, rows, HD)
    heads_k = keys.reshape(seqs, rows, KVH, HD).transpose(0, 2, 1, 3)
    heads_v = values.reshape(seqs, rows, KVH, HD).transpose(0, 2, 1, 3)
    both_kv = jnp.stack([heads_k, heads_v], axis=2).reshape(pairs, rows, HD)
    local_q, received = sent_together((heads_q, both_kv), TP, 0, 1, 2)
    other = partner(received, TP, 0)
    is_even = lax.axis_index(TP) % 2 == 0
    local_k = jnp.where(is_even, received, other)
    local_v = jnp.where(is_even, other, received)
    pair_ids = lax.axis_index(TP) * owned + jnp.arange(owned, dtype=jnp.int32)
    seq_ids = pair_ids // HEADS
    matches = seq_ids[:, None] == jnp.arange(seqs, dtype=jnp.int32)[None, :]
    valid = jnp.sum(jnp.where(matches, lengths[None, :], 0), axis=1)
    output = attend_all(local_q, local_k, local_v, valid)
    returned = core_and_chips(output, ("tp_0", "tp_1"), (1, 0), 1, 0)
    return (
        returned.reshape(seqs, HEADS, rows, HD)
        .transpose(0, 2, 1, 3)
        .reshape(seqs, rows, HEADS * HD)
    )


def solution(mesh):
    torus = Mesh(mesh.devices.reshape(mesh.shape["groups"], 32, 2), ("groups", "tp_0", "tp_1"))
    placed = (P("groups", TP, None), P("groups", TP, None), P("groups", TP, None), P("groups"))
    return jax.shard_map(
        per_device, mesh=torus, in_specs=placed, out_specs=P("groups", TP, None), check_vma=False
    )
```

profile of v0, /device:TPU:228, one launch (start us, length us, event | category | flops | bytes accessed | tf_op | source)
XLA Modules:
  0.0 383.1 jit_solution(45898778117336338)
XLA Ops:
  0.0 1.1 copy.18
  1.2 1.1 copy.17
  2.9 0.6 copy-done
  4.3 1.7 pad_maximum_fusion
  6.0 31.6 %all-to-all-start = ((bf16[64,64,256]{2,1,0:T(8,128)(2,1)}), bf16[64,64,256]{2,1,0:T(8,128)(2,1)S(1)}, u32[]{:S(2)}, u32[]{:S(2)}) async-start(bf16[64,64,256]{2,1,0:T(8,128)(2,1)} %pad_maximum_fusion), calls=%async_computation | async-start | bytes 4194304 | tf_op jit(solution)/shard_map/all_to_all | solution.py:20
  37.6 0.7 fusion.130
  42.6 189.1 %all-to-all-done = bf16[64,64,256]{2,1,0:T(8,128)(2,1)S(1)} async-done(((bf16[64,64,256]{2,1,0:T(8,128)(2,1)}), bf16[64,64,256]{2,1,0:T(8,128)(2,1)S(1)}, u32[]{:S(2)}, u32[]{:S(2)}) %all-to-all-start) | async-done | bytes 2097184 | tf_op jit(solution)/shard_map/all_to_all | solution.py:20
  231.8 1.0 slice.102
  236.5 1.1 fusion.132
  237.7 1.6 fusion.133
  239.2 2.0 fusion.134
  241.3 2.9 fusion.135
  244.2 3.2 fusion.136
  247.5 3.7 fusion.137
  251.2 4.2 %fusion.138 = (f32[512]{0:T(512)S(1)}, bf16[512,4096]{1,0:T(8,128)(2,1)S(1)}) fusion(bf16[1,4096,128]{2,1,0:T(8,128)(2,1)S(1)} %get-tuple-element.6, bf16[1,4096,256]{2,1,0:T(8,128)(2,1)S(1)} %bitcast.193, pred[4096]{0:T(1024)(128)(4,1)S(1)} %iota_compare_fusion.8, s32[512]{0:T(512)S(1)} %iota_add_fusion), kind=kOutput, calls=%fused_computation.149 | convolution fusion | flops 551550464 | bytes 5382144 | tf_op jit(solution)/shard_map/gqd,gkd->gqk/dot_general | solution.py:64
  256.2 0.6 fusion.108
  256.9 0.8 fusion.88
  257.6 0.9 fusion.100
  258.5 1.0 fusion.120
  259.6 1.2 fusion.94
  260.8 1.3 fusion.114
  262.2 4.6 %all_to_all.22 = bf16[32,2,1,64,128]{4,3,0,2,1:T(8,128)(2,1)S(1)} all-to-all(bf16[32,2,1,64,128]{4,3,0,2,1:T(8,128)(2,1)S(1)} %copy.12), channel_id=1, replica_groups=mesh['groups'=4,'tp_0'=32,'tp_1'=2] {'tp_1'}, dimensions={1} | all-to-all | bytes 2097152 | tf_op jit(solution)/shard_map/all_to_all | solution.py:50
  266.9 114.9 %all_to_all.23 = bf16[32,2,1,64,128]{4,3,1,2,0:T(8,128)(2,1)S(1)} all-to-all(bf16[32,2,1,64,128]{4,3,1,2,0:T(8,128)(2,1)S(1)} %copy.13), channel_id=1, replica_groups=mesh['groups'=4,'tp_0'=32,'tp_1'=2] {'tp_0'}, dimensions={0} | all-to-all | bytes 2097152 | tf_op jit(solution)/shard_map/all_to_all | solution.py:50
  381.8 1.2 copy.20
  (36 shorter events, 10.2 us)
Async XLA Ops:
  2.3 1.2 copy-start
  6.0 31.7 %copy-start.1 = (s32[2]{0:T(128)S(1)}, s32[2]{0:T(128)}, u32[]{:S(2)}) copy-start(s32[2]{0:T(128)} %param.7) | copy-start | bytes 28
  6.0 225.8 %all-to-all-start = ((bf16[64,64,256]{2,1,0:T(8,128)(2,1)}), bf16[64,64,256]{2,1,0:T(8,128)(2,1)S(1)}, u32[]{:S(2)}, u32[]{:S(2)}) async-start(bf16[64,64,256]{2,1,0:T(8,128)(2,1)} %pad_maximum_fusion), calls=%async_computation | async-start | bytes 4194304 | tf_op jit(solution)/shard_map/all_to_all | solution.py:20
  232.8 3.2 collective-permute-start
where the time goes:
time: 390 us; the launch traced here: 383 us
  waiting for transfers between devices  189 us (48%)
  blocking collectives  120 us (31%)
  starting transfers between devices  31.6 us (8%)
  matrix products  25.9 us (7%)
  other arithmetic  9.96 us (3%)
  local copies, waits for them, and re-layouts  6.55 us (2%)
    all_to_all x1, waiting for transfers between devices, sent_together(): lax.all_to_all(both, axis, split_axis=split_dim, concat_axis=concat_dim,...  189 us
    all_to_all x2, blocking collectives, moved_by_axis(): result = lax.all_to_all(result, axes[k], k, k, tiled=True)  120 us
    all_to_all x1, starting transfers between devices, sent_together(): lax.all_to_all(both, axis, split_axis=split_dim, concat_axis=concat_dim,...  31.6 us
    dot_general x8, matrix products, block_attend(): jnp.einsum('gqd,gkd->gqk', block_q, key_rows, preferred_element_type=jnp....  19.2 us
  transfers between devices with their start and end apart: 2, of which 1 were waited for; matrix products, arithmetic and copies ran while one was open for 2% of the time, Pallas kernels for 0%

commit v1 on v0

v1 whole, which is shorter than its diff:
```python
import functools

import jax
import jax.numpy as jnp
from jax import lax
from jax.experimental import pallas as pl
from jax.experimental.pallas import tpu as pltpu
from jax.sharding import Mesh
from jax.sharding import PartitionSpec as P

HEADS = 32
KVH = 16
HD = 128
SHARED = HEADS // KVH
CORES = 2
RING, CORE = "tp_0", "tp_1"

query_scale = 144.0 ** (-0.5)
soft_cap = 50.0
tanh_scale = query_scale / soft_cap
exp_scale = soft_cap * 1.4426950408889634

TILE_CHUNKS = 4


def vmem():
    return pl.BlockSpec(memory_space=pltpu.VMEM)


def smem():
    return pl.BlockSpec(memory_space=pltpu.SMEM)


def first_rows(count, lanes):
    return pl.BlockSpec((count, lanes), lambda i: (0, 0))


def pack(queries, keys, values, place):
    seqs, rows, _ = queries.shape
    chips = seqs * KVH
    half = chips // 2
    wide = SHARED * HD
    length = (half - 1) * rows + rows // 2

    def body(place_ref, q_ref, k_ref, v_ref, kv_up, kv_down, q_up, q_down, kv_own, q_own):
        me = place_ref[0]
        for slot in range(chips):
            owner = lax.rem(me + slot, chips)
            seq = owner // KVH
            head = lax.rem(owner, KVH)
            q = q_ref[seq, :, pl.ds(pl.multiple_of(head * wide, wide), wide)]
            k = k_ref[seq, :, pl.ds(pl.multiple_of(head * HD, HD), HD)]
            v = v_ref[seq, :, pl.ds(pl.multiple_of(head * HD, HD), HD)]
            if slot == 0:
                q_own[...] = q
                kv_own[:, :HD] = k
                kv_own[:, HD:] = v
            elif slot == half:
                mid = rows // 2
                at = (half - 1) * rows
                q_up[at:, :] = q[:mid]
                kv_up[at:, :HD] = k[:mid]
                kv_up[at:, HD:] = v[:mid]
                q_down[at:, :] = q[mid:]
                kv_down[at:, :HD] = k[mid:]
                kv_down[at:, HD:] = v[mid:]
            else:
                q_to, kv_to, step = (q_up, kv_up, slot) if slot < half else (q_down, kv_down, chips - slot)
                at = (step - 1) * rows
                q_to[at : at + rows, :] = q
                kv_to[at : at + rows, :HD] = k
                kv_to[at : at + rows, HD:] = v

    long = jax.ShapeDtypeStruct((length, wide), queries.dtype)
    short = jax.ShapeDtypeStruct((rows, wide), queries.dtype)
    return pl.pallas_call(
        body,
        grid=(1,),
        out_shape=(long, long, long, long, short, short),
        in_specs=[smem(), vmem(), vmem(), vmem()],
        out_specs=[vmem()] * 6,
        name="pack",
    )(place, queries, keys, values)


def gather_blocks(q_parts, kv_parts, partner_parts, place, rows, chips):
    half = chips // 2
    wide = SHARED * HD
    count = len(q_parts)
    slots = [0] + [s for k in range(1, half) for s in (k, chips - k)] + [half, half]

    def body(place_ref, *refs):
        q_refs = refs[:count]
        kv_refs = refs[count : 2 * count]
        other_refs = refs[2 * count : 2 * count + len(partner_parts)]
        q_out, k_out, v_out = refs[2 * count + len(partner_parts) :]
        me = place_ref[0]
        core = place_ref[1]
        which, inside = 0, 0
        for i in range(count):
            slot = (chips - slots[i]) % chips
            size = q_parts_rows[i]
            shift = rows // 2 if i == count - 1 else 0
            chunk = lax.rem(me + slot, chips)
            at = pl.multiple_of(chunk * rows + shift, rows // 2)
            for h in range(SHARED):
                q_out[h, pl.ds(at, size), :] = q_refs[i][:size, h * HD : (h + 1) * HD]
            base = pl.multiple_of((chunk * CORES + core) * rows + shift, rows // 2)
            k_out[pl.ds(base, size), :] = kv_refs[i][:size, :HD]
            v_out[pl.ds(base, size), :] = kv_refs[i][:size, HD:]
            if inside >= other_refs[which].shape[0]:
                which, inside = which + 1, 0
            base = pl.multiple_of((chunk * CORES + 1 - core) * rows + shift, rows // 2)
            k_out[pl.ds(base, size), :] = other_refs[which][inside : inside + size, :HD]
            v_out[pl.ds(base, size), :] = other_refs[which][inside : inside + size, HD:]
            inside += size

    q_parts_rows = [rows] * (count - 2) + [rows // 2] * 2
    specs = [first_rows(q_parts_rows[i], wide) for i in range(count)]
    out = (
        jax.ShapeDtypeStruct((SHARED, chips * rows, HD), q_parts[0].dtype),
        jax.ShapeDtypeStruct((chips * CORES * rows, HD), q_parts[0].dtype),
        jax.ShapeDtypeStruct((chips * CORES * rows, HD), q_parts[0].dtype),
    )
    return pl.pallas_call(
        body,
        grid=(1,),
        out_shape=out,
        in_specs=[smem()] + specs + specs + [vmem()] * len(partner_parts),
        out_specs=[vmem()] * 3,
        name="gather_blocks",
    )(place, *q_parts, *kv_parts, *partner_parts)


def attend(q_all, keys, values, place, head, rows, chips):
    half = chips // 2
    tile = TILE_CHUNKS * rows
    span = tile * CORES
    tiles = chips // TILE_CHUNKS
    length = (half - 1) * rows + rows // 2

    def body(place_ref, q_ref, k_ref, v_ref, up, down, own, mixed_ref):
        me = place_ref[0]
        core = place_ref[1]
        valid = place_ref[2]
        row = lax.broadcasted_iota(jnp.int32, (tile, 1), 0)
        offset = (row // rows) * (rows * CORES) + core * rows + lax.rem(row, rows)

        def weights(q, index):
            k = k_ref[pl.ds(pl.multiple_of(index * span, span), span), :]
            score = lax.dot_general(q, k, (((1,), (1,)), ((), ())), preferred_element_type=jnp.float32)
            return jnp.exp2(jnp.tanh(score * tanh_scale) * exp_scale)

        def mix(weight, index):
            v = v_ref[pl.ds(pl.multiple_of(index * span, span), span), :]
            return lax.dot_general(
                weight.astype(jnp.bfloat16), v, (((1,), (0,)), ((), ())), preferred_element_type=jnp.float32
            )

        def one_tile(index, carry):
            first = index * span

            @pl.when(first < valid)
            def _():
                q = q_ref[0, pl.ds(pl.multiple_of(index * tile, tile), tile), :]

                def step(j, state):
                    acc, total = state
                    weight = weights(q, j)
                    return acc + mix(weight, j), total + jnp.sum(weight, axis=1, keepdims=True)

                start = (jnp.zeros((tile, HD), jnp.float32), jnp.zeros((tile, 1), jnp.float32))
                acc, total = lax.fori_loop(0, index, step, start)
                key = lax.broadcasted_iota(jnp.int32, (tile, span), 1)
                weight = jnp.where(key <= offset, weights(q, index), 0.0)
                total = total + jnp.sum(weight, axis=1, keepdims=True)
                acc = acc + mix(weight, index)
                live = first + offset < valid
                result = jnp.where(live, acc / total, 0.0).astype(jnp.bfloat16)
                mixed_ref[pl.ds(pl.multiple_of(index * tile, tile), tile), :] = result

            @pl.when(first >= valid)
            def _():
                mixed_ref[pl.ds(pl.multiple_of(index * tile, tile), tile), :] = jnp.zeros((tile, HD), jnp.bfloat16)

            return carry

        lax.fori_loop(0, tiles, one_tile, 0)
        for slot in range(chips):
            chunk = lax.rem(me + slot, chips)
            block = mixed_ref[pl.ds(pl.multiple_of(chunk * rows, rows), rows), :]
            if slot == 0:
                own[...] = block
            elif slot == half:
                at = (half - 1) * rows
                up[at:, :] = block[: rows // 2]
                down[at:, :] = block[rows // 2 :]
            else:
                to, step = (up, slot) if slot < half else (down, chips - slot)
                to[(step - 1) * rows : step * rows, :] = block

    long = jax.ShapeDtypeStruct((length, HD), q_all.dtype)
    short = jax.ShapeDtypeStruct((rows, HD), q_all.dtype)
    return pl.pallas_call(
        body,
        grid=(1,),
        out_shape=(long, long, short),
        in_specs=[smem(), pl.BlockSpec((1, chips * rows, HD), lambda i: (head, 0, 0)), vmem(), vmem()],
        out_specs=[vmem()] * 3,
        scratch_shapes=[pltpu.VMEM((chips * rows, HD), jnp.bfloat16)],
        name=f"attend_{head}",
    )(place, q_all, keys, values)


def unpack(parts, place, seqs, rows):
    chips = seqs * KVH
    half = chips // 2
    count = len(parts[0])
    slots = [0] + [s for k in range(1, half) for s in (k, chips - k)] + [half, half]
    sizes = [rows] * (count - 2) + [rows // 2] * 2

    def body(place_ref, *refs):
        out = refs[-1]
        me = place_ref[0]
        for i in range(count):
            owner = lax.rem(me + (chips - slots[i]) % chips, chips)
            seq = owner // KVH
            head = lax.rem(owner, KVH)
            start = rows // 2 if i == count - 1 else 0
            for h in range(SHARED):
                at = pl.multiple_of((head * SHARED + h) * HD, HD)
                out[seq, start : start + sizes[i], pl.ds(at, HD)] = refs[h * count + i][...]

    specs = [first_rows(sizes[i], HD) for i in range(count)]
    return pl.pallas_call(
        body,
        grid=(1,),
        out_shape=jax.ShapeDtypeStruct((seqs, rows, HEADS * HD), parts[0][0].dtype),
        in_specs=[smem()] + specs * SHARED,
        out_specs=vmem(),
        name="unpack",
    )(place, *[p for part in parts for p in part])


def shifted(value, by):
    chips = lax.axis_size(RING)
    return lax.ppermute(value, RING, [(i, (i + by) % chips) for i in range(chips)])


def pass_on(chains, rows, each_step=None):
    arrived = [[] for _ in chains]
    rest = list(chains)
    done = []
    step = 0
    while rest[0][0].shape[0]:
        step += 1
        for i in range(len(chains)):
            up, down = rest[i]
            if len(done) >= 3:
                up, down, _ = lax.optimization_barrier((up, down, done[-3]))
            got = lax.optimization_barrier((shifted(up, 1), shifted(down, -1)))
            done.append(got)
            arrived[i].extend(got)
            size = min(rows, up.shape[0])
            rest[i] = tuple(g[size:] for g in got)
        if each_step is not None:
            each_step(step, arrived)
    return arrived


def per_device(queries, keys, values, lengths):
    seqs, rows, _ = queries.shape
    chips = lax.axis_size(RING)
    half = chips // 2
    me = lax.axis_index(RING)
    core = lax.axis_index(CORE)
    valid = lax.dynamic_index_in_dim(lengths, me // KVH, keepdims=False)
    place = jnp.stack([me, core, valid]).astype(jnp.int32)
    kv_up, kv_down, q_up, q_down, kv_own, q_own = pack(queries, keys, values, place)

    swapped = []
    state = {"from": 0}

    def each_step(step, arrived):
        if step not in (half // 3, 2 * half // 3, half - 2, half):
            return
        blocks = ([kv_own] if not swapped else []) + [
            b[: min(rows, b.shape[0])] for b in arrived[0][state["from"] :]
        ]
        state["from"] = len(arrived[0])
        joined = jnp.concatenate(blocks, axis=0)
        swapped.append(lax.ppermute(joined, CORE, [(0, 1), (1, 0)]))

    kv_got, q_got = pass_on([(kv_up, kv_down), (q_up, q_down)], rows, each_step)
    q_all, k_all, v_all = gather_blocks([q_own] + q_got, [kv_own] + kv_got, swapped, place, rows, chips)
    results = [attend(q_all, k_all, v_all, place, h, rows, chips) for h in range(SHARED)]
    back = pass_on([(up, down) for up, down, _ in results], rows)
    parts = [[results[h][2]] + back[h] for h in range(SHARED)]
    return unpack(parts, place, seqs, rows)


def solution(mesh):
    groups = mesh.shape["groups"]
    torus = Mesh(mesh.devices.reshape(groups, -1, CORES), ("groups", RING, CORE))
    placed = P("groups", (RING, CORE), None)
    return jax.shard_map(
        per_device, mesh=torus, in_specs=(placed, placed, placed, P("groups")), out_specs=placed, check_vma=False
    )
```

time: 390 us -> 441 us (1.13); the launches traced: 383 us -> 439 us
  starting transfers between devices: 31.6 us -> 239 us
  blocking collectives: 120 us -> 0 us
  waiting for transfers between devices: 189 us -> 116 us
  Pallas kernels: 0 us -> 47.9 us
  matrix products: 25.9 us -> 0 us
  local copies, waits for them, and re-layouts: 6.55 us -> 32.3 us
  other arithmetic: 9.96 us -> 1.19 us
    ppermute x1 -> x132, starting transfers between devices: 0.01 us -> 239 us  [the longest x128 239 us: shifted(): lax.ppermute(value, RING, [(i, (i + by) % chips) for i in range(chips)])]
    all_to_all x1 -> x0, waiting for transfers between devices: 189 us -> none  [sent_together(): lax.all_to_all(both, axis, split_axis=split_dim, concat_axis=concat_dim,...]
    all_to_all x2 -> x0, blocking collectives: 120 us -> none  [moved_by_axis(): result = lax.all_to_all(result, axes[k], k, k, tiled=True)]
    ppermute x1 -> x132, waiting for transfers between devices: 0.01 us -> 116 us  [the longest x128 116 us: shifted(): lax.ppermute(value, RING, [(i, (i + by) % chips) for i in range(chips)])]
    pallas_call x0 -> x5, Pallas kernels: none -> 47.9 us  [the longest x2 37.9 us: attend(): pl.pallas_call(body, grid=(1,), out_shape=(long, long, short), in_specs=[...]
    all_to_all x1 -> x0, starting transfers between devices: 31.6 us -> none  [sent_together(): lax.all_to_all(both, axis, split_axis=split_dim, concat_axis=concat_dim,...]
    unnamed x7 -> x294, local copies, waits for them, and re-layouts: 3.18 us -> 30.1 us
    dot_general x16 -> x0, matrix products: 25.9 us -> none  [the longest x8 19.2 us: block_attend(): jnp.einsum('gqd,gkd->gqk', block_q, key_rows, preferred_element_type=jnp....]
  transfers between devices with their start and end apart: 2 -> 132, of which waited for: 1 -> 62; matrix products, arithmetic and copies ran while one was open for 2% -> 0% of each run, Pallas kernels for 0% -> 4%
where the time goes in v1:
time: 441 us; the launch traced here: 439 us
  starting transfers between devices  239 us (54%)
  waiting for transfers between devices  116 us (26%)
  Pallas kernels  47.9 us (11%)
  local copies, waits for them, and re-layouts  32.3 us (7%)
    ppermute x128, starting transfers between devices, shifted(): lax.ppermute(value, RING, [(i, (i + by) % chips) for i in range(chips)])  239 us
    ppermute x128, waiting for transfers between devices, shifted(): lax.ppermute(value, RING, [(i, (i + by) % chips) for i in range(chips)])  116 us
    pallas_call x2, Pallas kernels, attend(): pl.pallas_call(body, grid=(1,), out_shape=(long, long, short), in_specs=[...  37.9 us
    unnamed x294, local copies, waits for them, and re-layouts  30.1 us
  transfers between devices with their start and end apart: 132, of which 62 were waited for; matrix products, arithmetic and copies ran while one was open for 0% of the time, Pallas kernels for 4%

profile of v1, /device:TPU:228, one launch (start us, length us, event | category | flops | bytes accessed | tf_op | source)
XLA Modules:
  0.0 438.6 jit_solution(12595979585266808092)
XLA Ops:
  5.7 3.3 collective-permute-start
  12.3 9.0 %collective-permute-done.refs_1_ = bf16[992,256]{1,0:T(8,128)(2,1)S(1)} collective-permute-done((bf16[992,256]{1,0:T(8,128)(2,1)}, bf16[992,256]{1,0:T(8,128)(2,1)S(1)}, u32[]{:S(2)}, u32[]{:S(2)}) %collective-permute-start) | collective-permute-done | bytes 507936 | tf_op jit(solution)/shard_map/ppermute | solution.py:247
  21.3 3.6 collective-permute-done.1.refs_2_
  25.7 5.5 %collective-permute-done.2.refs_34_ = bf16[992,256]{1,0:T(8,128)(2,1)S(1)} collective-permute-done((bf16[992,256]{1,0:T(8,128)(2,1)}, bf16[992,256]{1,0:T(8,128)(2,1)S(1)}, u32[]{:S(2)}, u32[]{:S(2)}) %collective-permute-start.2) | collective-permute-done | bytes 507936 | tf_op jit(solution)/shard_map/ppermute | solution.py:247
  38.2 4.5 %collective-permute-start.5 = (bf16[928,256]{1,0:T(8,128)(2,1)S(1)}, bf16[928,256]{1,0:T(8,128)(2,1)S(1)}, u32[]{:S(2)}, u32[]{:S(2)}) collective-permute-start(bf16[928,256]{1,0:T(8,128)(2,1)S(1)} %slice.451), channel_id=1, source_target_pairs={{0,62},{2,0},{4,2},{6,4},{8,6},{10,8},{12,10},{14,12},{16,14},{18,... | collective-permute-start | bytes 1425416 | tf_op jit(solution)/shard_map/ppermute | solution.py:247
  42.7 6.8 %collective-permute-done.7.refs_37_ = bf16[928,256]{1,0:T(8,128)(2,1)S(1)} collective-permute-done((bf16[928,256]{1,0:T(8,128)(2,1)S(1)}, bf16[928,256]{1,0:T(8,128)(2,1)S(1)}, u32[]{:S(2)}, u32[]{:S(2)}) %collective-permute-start.7) | collective-permute-done | bytes 475168 | tf_op jit(solution)/shard_map/ppermute | solution.py:247
  49.6 4.8 %collective-permute-done.6.refs_36_ = bf16[928,256]{1,0:T(8,128)(2,1)S(1)} collective-permute-done((bf16[928,256]{1,0:T(8,128)(2,1)S(1)}, bf16[928,256]{1,0:T(8,128)(2,1)S(1)}, u32[]{:S(2)}, u32[]{:S(2)}) %collective-permute-start.6) | collective-permute-done | bytes 475168 | tf_op jit(solution)/shard_map/ppermute | solution.py:247
  54.6 8.8 %collective-permute-start.11 = (bf16[864,256]{1,0:T(8,128)(2,1)S(1)}, bf16[864,256]{1,0:T(8,128)(2,1)S(1)}, u32[]{:S(2)}, u32[]{:S(2)}) collective-permute-start(bf16[864,256]{1,0:T(8,128)(2,1)S(1)} %slice.459), channel_id=1, source_target_pairs={{0,62},{2,0},{4,2},{6,4},{8,6},{10,8},{12,10},{14,12},{16,14},{18,... | collective-permute-start | bytes 1327112 | tf_op jit(solution)/shard_map/ppermute | solution.py:247
  64.5 9.9 %collective-permute-start.9 = (bf16[864,256]{1,0:T(8,128)(2,1)S(1)}, bf16[864,256]{1,0:T(8,128)(2,1)S(1)}, u32[]{:S(2)}, u32[]{:S(2)}) collective-permute-start(bf16[864,256]{1,0:T(8,128)(2,1)S(1)} %slice.453), channel_id=1, source_target_pairs={{0,62},{2,0},{4,2},{6,4},{8,6},{10,8},{12,10},{14,12},{16,14},{18,... | collective-permute-start | bytes 1327112 | tf_op jit(solution)/shard_map/ppermute | solution.py:247
  74.6 8.8 %collective-permute-start.15 = (bf16[800,256]{1,0:T(8,128)(2,1)S(1)}, bf16[800,256]{1,0:T(8,128)(2,1)S(1)}, u32[]{:S(2)}, u32[]{:S(2)}) collective-permute-start(bf16[800,256]{1,0:T(8,128)(2,1)S(1)} %slice.463), channel_id=1, source_target_pairs={{0,62},{2,0},{4,2},{6,4},{8,6},{10,8},{12,10},{14,12},{16,14},{18,... | collective-permute-start | bytes 1228808 | tf_op jit(solution)/shard_map/ppermute | solution.py:247
  84.3 8.9 %collective-permute-start.13 = (bf16[800,256]{1,0:T(8,128)(2,1)S(1)}, bf16[800,256]{1,0:T(8,128)(2,1)S(1)}, u32[]{:S(2)}, u32[]{:S(2)}) collective-permute-start(bf16[800,256]{1,0:T(8,128)(2,1)S(1)} %slice.457), channel_id=1, source_target_pairs={{0,62},{2,0},{4,2},{6,4},{8,6},{10,8},{12,10},{14,12},{16,14},{18,... | collective-permute-start | bytes 1228808 | tf_op jit(solution)/shard_map/ppermute | solution.py:247
  93.4 7.9 %collective-permute-start.19 = (bf16[736,256]{1,0:T(8,128)(2,1)S(1)}, bf16[736,256]{1,0:T(8,128)(2,1)S(1)}, u32[]{:S(2)}, u32[]{:S(2)}) collective-permute-start(bf16[736,256]{1,0:T(8,128)(2,1)S(1)} %slice.467), channel_id=1, source_target_pairs={{0,62},{2,0},{4,2},{6,4},{8,6},{10,8},{12,10},{14,12},{16,14},{18,... | collective-permute-start | bytes 1130504 | tf_op jit(solution)/shard_map/ppermute | solution.py:247
  102.3 8.4 %collective-permute-start.17 = (bf16[736,256]{1,0:T(8,128)(2,1)S(1)}, bf16[736,256]{1,0:T(8,128)(2,1)S(1)}, u32[]{:S(2)}, u32[]{:S(2)}) collective-permute-start(bf16[736,256]{1,0:T(8,128)(2,1)S(1)} %slice.461), channel_id=1, source_target_pairs={{0,62},{2,0},{4,2},{6,4},{8,6},{10,8},{12,10},{14,12},{16,14},{18,... | collective-permute-start | bytes 1130504 | tf_op jit(solution)/shard_map/ppermute | solution.py:247
  111.0 7.2 %collective-permute-start.23 = (bf16[672,256]{1,0:T(8,128)(2,1)S(1)}, bf16[672,256]{1,0:T(8,128)(2,1)S(1)}, u32[]{:S(2)}, u32[]{:S(2)}) collective-permute-start(bf16[672,256]{1,0:T(8,128)(2,1)S(1)} %slice.471), channel_id=1, source_target_pairs={{0,62},{2,0},{4,2},{6,4},{8,6},{10,8},{12,10},{14,12},{16,14},{18,... | collective-permute-start | bytes 1032200 | tf_op jit(solution)/shard_map/ppermute | solution.py:247
  119.1 7.8 %collective-permute-start.21 = (bf16[672,256]{1,0:T(8,128)(2,1)S(1)}, bf16[672,256]{1,0:T(8,128)(2,1)S(1)}, u32[]{:S(2)}, u32[]{:S(2)}) collective-permute-start(bf16[672,256]{1,0:T(8,128)(2,1)S(1)} %slice.465), channel_id=1, source_target_pairs={{0,62},{2,0},{4,2},{6,4},{8,6},{10,8},{12,10},{14,12},{16,14},{18,... | collective-permute-start | bytes 1032200 | tf_op jit(solution)/shard_map/ppermute | solution.py:247
  127.3 6.4 %collective-permute-start.27 = (bf16[608,256]{1,0:T(8,128)(2,1)S(1)}, bf16[608,256]{1,0:T(8,128)(2,1)S(1)}, u32[]{:S(2)}, u32[]{:S(2)}) collective-permute-start(bf16[608,256]{1,0:T(8,128)(2,1)S(1)} %slice.475), channel_id=1, source_target_pairs={{0,62},{2,0},{4,2},{6,4},{8,6},{10,8},{12,10},{14,12},{16,14},{18,... | collective-permute-start | bytes 933896 | tf_op jit(solution)/shard_map/ppermute | solution.py:247
  134.6 15.6 %collective-permute-start.25 = (bf16[608,256]{1,0:T(8,128)(2,1)S(1)}, bf16[608,256]{1,0:T(8,128)(2,1)S(1)}, u32[]{:S(2)}, u32[]{:S(2)}) collective-permute-start(bf16[608,256]{1,0:T(8,128)(2,1)S(1)} %slice.469), channel_id=1, source_target_pairs={{0,62},{2,0},{4,2},{6,4},{8,6},{10,8},{12,10},{14,12},{16,14},{18,... | collective-permute-start | bytes 933896 | tf_op jit(solution)/shard_map/ppermute | solution.py:247
  153.6 4.3 collective-permute-done.25.refs_14_
  181.1 3.4 collective-permute-start.37
  221.9 3.4 collective-permute-start.59
  250.8 4.3 gather_blocks.1
  255.1 19.0 %attend_0.1 = (bf16[992,128]{1,0:T(8,128)(2,1)}, bf16[992,128]{1,0:T(8,128)(2,1)}, bf16[64,128]{1,0:T(8,128)(2,1)}) custom-call(s32[3]{0:T(128)} %pad_add_fusion.place_ref, bf16[2,2048,128]{2,1,0:T(8,128)(2,1)} %get-tuple-element.392.q_ref, bf16[4096,128]{1,0:T(8,128)(2,1)} %get-tuple-element.393.k_ref, bf16[4096,128]{1,0:T(8,128)(2,1)} %get-tuple-element.394.v_ref), custom_call_target="tpu_custom_call" | custom-call | tf_op jit(solution)/shard_map/attend_0/pallas_call | solution.py:204
  276.2 19.0 %attend_1.1 = (bf16[992,128]{1,0:T(8,128)(2,1)}, bf16[992,128]{1,0:T(8,128)(2,1)}, bf16[64,128]{1,0:T(8,128)(2,1)}) custom-call(s32[3]{0:T(128)} %pad_add_fusion.place_ref, bf16[2,2048,128]{2,1,0:T(8,128)(2,1)} %get-tuple-element.392.q_ref, bf16[4096,128]{1,0:T(8,128)(2,1)} %get-tuple-element.393.k_ref, bf16[4096,128]{1,0:T(8,128)(2,1)} %get-tuple-element.394.v_ref), custom_call_target="tpu_custom_call" | custom-call | tf_op jit(solution)/shard_map/attend_1/pallas_call | solution.py:204
  353.4 3.8 collective-permute-done.93.refs_45_
  (668 shorter events, 252.2 us)
Async XLA Ops:
  9.0 22.1 %collective-permute-start.2 = (bf16[992,256]{1,0:T(8,128)(2,1)}, bf16[992,256]{1,0:T(8,128)(2,1)S(1)}, u32[]{:S(2)}, u32[]{:S(2)}) collective-permute-start(bf16[992,256]{1,0:T(8,128)(2,1)} %get-tuple-element.269), channel_id=1, source_target_pairs={{0,2},{2,4},{4,6},{6,8},{8,10},{10,12},{12,14},{14,16},{16,18},{18... | collective-permute-start | bytes 1523720 | tf_op jit(solution)/shard_map/ppermute | solution.py:247
  12.3 22.2 %collective-permute-start.3 = (bf16[992,256]{1,0:T(8,128)(2,1)}, bf16[992,256]{1,0:T(8,128)(2,1)S(1)}, u32[]{:S(2)}, u32[]{:S(2)}) collective-permute-start(bf16[992,256]{1,0:T(8,128)(2,1)} %get-tuple-element.270), channel_id=1, source_target_pairs={{0,62},{2,0},{4,2},{6,4},{8,6},{10,8},{12,10},{14,12},{16,14},{18,... | collective-permute-start | bytes 1523720 | tf_op jit(solution)/shard_map/ppermute | solution.py:247
  34.7 19.7 %collective-permute-start.6 = (bf16[928,256]{1,0:T(8,128)(2,1)S(1)}, bf16[928,256]{1,0:T(8,128)(2,1)S(1)}, u32[]{:S(2)}, u32[]{:S(2)}) collective-permute-start(bf16[928,256]{1,0:T(8,128)(2,1)S(1)} %slice.454), channel_id=1, source_target_pairs={{0,2},{2,4},{4,6},{6,8},{8,10},{10,12},{12,14},{14,16},{16,18},{18... | collective-permute-start | bytes 1425416 | tf_op jit(solution)/shard_map/ppermute | solution.py:247
  37.9 25.6 %collective-permute-start.4 = (bf16[928,256]{1,0:T(8,128)(2,1)S(1)}, bf16[928,256]{1,0:T(8,128)(2,1)S(1)}, u32[]{:S(2)}, u32[]{:S(2)}) collective-permute-start(bf16[928,256]{1,0:T(8,128)(2,1)S(1)} %slice.450), channel_id=1, source_target_pairs={{0,2},{2,4},{4,6},{6,8},{8,10},{10,12},{12,14},{14,16},{16,18},{18... | collective-permute-start | bytes 1425416 | tf_op jit(solution)/shard_map/ppermute | solution.py:247
  38.2 25.3 %collective-permute-start.5 = (bf16[928,256]{1,0:T(8,128)(2,1)S(1)}, bf16[928,256]{1,0:T(8,128)(2,1)S(1)}, u32[]{:S(2)}, u32[]{:S(2)}) collective-permute-start(bf16[928,256]{1,0:T(8,128)(2,1)S(1)} %slice.451), channel_id=1, source_target_pairs={{0,62},{2,0},{4,2},{6,4},{8,6},{10,8},{12,10},{14,12},{16,14},{18,... | collective-permute-start | bytes 1425416 | tf_op jit(solution)/shard_map/ppermute | solution.py:247
  54.5 19.9 %collective-permute-start.10 = (bf16[864,256]{1,0:T(8,128)(2,1)S(1)}, bf16[864,256]{1,0:T(8,128)(2,1)S(1)}, u32[]{:S(2)}, u32[]{:S(2)}) collective-permute-start(bf16[864,256]{1,0:T(8,128)(2,1)S(1)} %slice.458), channel_id=1, source_target_pairs={{0,2},{2,4},{4,6},{6,8},{8,10},{10,12},{12,14},{14,16},{16,18},{18... | collective-permute-start | bytes 1327112 | tf_op jit(solution)/shard_map/ppermute | solution.py:247
  54.6 19.7 %collective-permute-start.11 = (bf16[864,256]{1,0:T(8,128)(2,1)S(1)}, bf16[864,256]{1,0:T(8,128)(2,1)S(1)}, u32[]{:S(2)}, u32[]{:S(2)}) collective-permute-start(bf16[864,256]{1,0:T(8,128)(2,1)S(1)} %slice.459), channel_id=1, source_target_pairs={{0,62},{2,0},{4,2},{6,4},{8,6},{10,8},{12,10},{14,12},{16,14},{18,... | collective-permute-start | bytes 1327112 | tf_op jit(solution)/shard_map/ppermute | solution.py:247
  64.5 18.9 %collective-permute-start.8 = (bf16[864,256]{1,0:T(8,128)(2,1)S(1)}, bf16[864,256]{1,0:T(8,128)(2,1)S(1)}, u32[]{:S(2)}, u32[]{:S(2)}) collective-permute-start(bf16[864,256]{1,0:T(8,128)(2,1)S(1)} %slice.452), channel_id=1, source_target_pairs={{0,2},{2,4},{4,6},{6,8},{8,10},{10,12},{12,14},{14,16},{16,18},{18... | collective-permute-start | bytes 1327112 | tf_op jit(solution)/shard_map/ppermute | solution.py:247
  64.5 18.9 %collective-permute-start.9 = (bf16[864,256]{1,0:T(8,128)(2,1)S(1)}, bf16[864,256]{1,0:T(8,128)(2,1)S(1)}, u32[]{:S(2)}, u32[]{:S(2)}) collective-permute-start(bf16[864,256]{1,0:T(8,128)(2,1)S(1)} %slice.453), channel_id=1, source_target_pairs={{0,62},{2,0},{4,2},{6,4},{8,6},{10,8},{12,10},{14,12},{16,14},{18,... | collective-permute-start | bytes 1327112 | tf_op jit(solution)/shard_map/ppermute | solution.py:247
  74.4 18.7 %collective-permute-start.14 = (bf16[800,256]{1,0:T(8,128)(2,1)S(1)}, bf16[800,256]{1,0:T(8,128)(2,1)S(1)}, u32[]{:S(2)}, u32[]{:S(2)}) collective-permute-start(bf16[800,256]{1,0:T(8,128)(2,1)S(1)} %slice.462), channel_id=1, source_target_pairs={{0,2},{2,4},{4,6},{6,8},{8,10},{10,12},{12,14},{14,16},{16,18},{18... | collective-permute-start | bytes 1228808 | tf_op jit(solution)/shard_map/ppermute | solution.py:247
  74.6 18.6 %collective-permute-start.15 = (bf16[800,256]{1,0:T(8,128)(2,1)S(1)}, bf16[800,256]{1,0:T(8,128)(2,1)S(1)}, u32[]{:S(2)}, u32[]{:S(2)}) collective-permute-start(bf16[800,256]{1,0:T(8,128)(2,1)S(1)} %slice.463), channel_id=1, source_target_pairs={{0,62},{2,0},{4,2},{6,4},{8,6},{10,8},{12,10},{14,12},{16,14},{18,... | collective-permute-start | bytes 1228808 | tf_op jit(solution)/shard_map/ppermute | solution.py:247
  84.3 17.1 %collective-permute-start.12 = (bf16[800,256]{1,0:T(8,128)(2,1)S(1)}, bf16[800,256]{1,0:T(8,128)(2,1)S(1)}, u32[]{:S(2)}, u32[]{:S(2)}) collective-permute-start(bf16[800,256]{1,0:T(8,128)(2,1)S(1)} %slice.456), channel_id=1, source_target_pairs={{0,2},{2,4},{4,6},{6,8},{8,10},{10,12},{12,14},{14,16},{16,18},{18... | collective-permute-start | bytes 1228808 | tf_op jit(solution)/shard_map/ppermute | solution.py:247
  84.3 17.1 %collective-permute-start.13 = (bf16[800,256]{1,0:T(8,128)(2,1)S(1)}, bf16[800,256]{1,0:T(8,128)(2,1)S(1)}, u32[]{:S(2)}, u32[]{:S(2)}) collective-permute-start(bf16[800,256]{1,0:T(8,128)(2,1)S(1)} %slice.457), channel_id=1, source_target_pairs={{0,62},{2,0},{4,2},{6,4},{8,6},{10,8},{12,10},{14,12},{16,14},{18,... | collective-permute-start | bytes 1228808 | tf_op jit(solution)/shard_map/ppermute | solution.py:247
  93.3 17.5 %collective-permute-start.18 = (bf16[736,256]{1,0:T(8,128)(2,1)S(1)}, bf16[736,256]{1,0:T(8,128)(2,1)S(1)}, u32[]{:S(2)}, u32[]{:S(2)}) collective-permute-start(bf16[736,256]{1,0:T(8,128)(2,1)S(1)} %slice.466), channel_id=1, source_target_pairs={{0,2},{2,4},{4,6},{6,8},{8,10},{10,12},{12,14},{14,16},{16,18},{18... | collective-permute-start | bytes 1130504 | tf_op jit(solution)/shard_map/ppermute | solution.py:247
  93.4 17.3 %collective-permute-start.19 = (bf16[736,256]{1,0:T(8,128)(2,1)S(1)}, bf16[736,256]{1,0:T(8,128)(2,1)S(1)}, u32[]{:S(2)}, u32[]{:S(2)}) collective-permute-start(bf16[736,256]{1,0:T(8,128)(2,1)S(1)} %slice.467), channel_id=1, source_target_pairs={{0,62},{2,0},{4,2},{6,4},{8,6},{10,8},{12,10},{14,12},{16,14},{18,... | collective-permute-start | bytes 1130504 | tf_op jit(solution)/shard_map/ppermute | solution.py:247
  126.9 123.0 %collective-permute-start.64 = (bf16[704,256]{1,0:T(8,128)(2,1)S(1)}, bf16[704,256]{1,0:T(8,128)(2,1)S(1)}, u32[]{:S(2)}, u32[]{:S(2)}) collective-permute-start(bf16[704,256]{1,0:T(8,128)(2,1)S(1)} %constant_dynamic-update-slice_fusion), channel_id=1, source_target_pairs={{0,1},{1,0},{2,3},{3,2},{4,5},{5,4},{6,7},{7,6},{8,9},{9,8},{10,11... | collective-permute-start | bytes 1081352 | tf_op jit(solution)/shard_map/ppermute | solution.py:292
  127.1 23.1 %collective-permute-start.26 = (bf16[608,256]{1,0:T(8,128)(2,1)S(1)}, bf16[608,256]{1,0:T(8,128)(2,1)S(1)}, u32[]{:S(2)}, u32[]{:S(2)}) collective-permute-start(bf16[608,256]{1,0:T(8,128)(2,1)S(1)} %slice.474), channel_id=1, source_target_pairs={{0,2},{2,4},{4,6},{6,8},{8,10},{10,12},{12,14},{14,16},{16,18},{18... | collective-permute-start | bytes 933896 | tf_op jit(solution)/shard_map/ppermute | solution.py:247
  127.3 23.0 %collective-permute-start.27 = (bf16[608,256]{1,0:T(8,128)(2,1)S(1)}, bf16[608,256]{1,0:T(8,128)(2,1)S(1)}, u32[]{:S(2)}, u32[]{:S(2)}) collective-permute-start(bf16[608,256]{1,0:T(8,128)(2,1)S(1)} %slice.475), channel_id=1, source_target_pairs={{0,62},{2,0},{4,2},{6,4},{8,6},{10,8},{12,10},{14,12},{16,14},{18,... | collective-permute-start | bytes 933896 | tf_op jit(solution)/shard_map/ppermute | solution.py:247
  134.5 19.1 %collective-permute-start.24 = (bf16[608,256]{1,0:T(8,128)(2,1)S(1)}, bf16[608,256]{1,0:T(8,128)(2,1)S(1)}, u32[]{:S(2)}, u32[]{:S(2)}) collective-permute-start(bf16[608,256]{1,0:T(8,128)(2,1)S(1)} %slice.468), channel_id=1, source_target_pairs={{0,2},{2,4},{4,6},{6,8},{8,10},{10,12},{12,14},{14,16},{16,18},{18... | collective-permute-start | bytes 933896 | tf_op jit(solution)/shard_map/ppermute | solution.py:247
  134.6 23.4 %collective-permute-start.25 = (bf16[608,256]{1,0:T(8,128)(2,1)S(1)}, bf16[608,256]{1,0:T(8,128)(2,1)S(1)}, u32[]{:S(2)}, u32[]{:S(2)}) collective-permute-start(bf16[608,256]{1,0:T(8,128)(2,1)S(1)} %slice.469), channel_id=1, source_target_pairs={{0,62},{2,0},{4,2},{6,4},{8,6},{10,8},{12,10},{14,12},{16,14},{18,... | collective-permute-start | bytes 933896 | tf_op jit(solution)/shard_map/ppermute | solution.py:247
  209.8 40.1 %collective-permute-start.65 = (bf16[640,256]{1,0:T(8,128)(2,1)S(1)}, bf16[640,256]{1,0:T(8,128)(2,1)S(1)}, u32[]{:S(2)}, u32[]{:S(2)}) collective-permute-start(bf16[640,256]{1,0:T(8,128)(2,1)S(1)} %constant_dynamic-update-slice_fusion.11), channel_id=1, source_target_pairs={{0,1},{1,0},{2,3},{3,2},{4,5},{5,4},{6,7},{7,6},{8,9},{9,8},{10,11... | collective-permute-start | bytes 983048 | tf_op jit(solution)/shard_map/ppermute | solution.py:292
  225.3 24.6 %collective-permute-start.66 = (bf16[512,256]{1,0:T(8,128)(2,1)S(1)}, bf16[512,256]{1,0:T(8,128)(2,1)S(1)}, u32[]{:S(2)}, u32[]{:S(2)}) collective-permute-start(bf16[512,256]{1,0:T(8,128)(2,1)S(1)} %constant_dynamic-update-slice_fusion.21), channel_id=1, source_target_pairs={{0,1},{1,0},{2,3},{3,2},{4,5},{5,4},{6,7},{7,6},{8,9},{9,8},{10,11... | collective-permute-start | bytes 786440 | tf_op jit(solution)/shard_map/ppermute | solution.py:292
  274.1 24.8 %collective-permute-start.68 = (bf16[992,128]{1,0:T(8,128)(2,1)}, bf16[992,128]{1,0:T(8,128)(2,1)S(1)}, u32[]{:S(2)}, u32[]{:S(2)}) collective-permute-start(bf16[992,128]{1,0:T(8,128)(2,1)} %get-tuple-element.396), channel_id=1, source_target_pairs={{0,2},{2,4},{4,6},{6,8},{8,10},{10,12},{12,14},{14,16},{16,18},{18... | collective-permute-start | bytes 761864 | tf_op jit(solution)/shard_map/ppermute | solution.py:247
  274.9 24.0 %collective-permute-start.69 = (bf16[992,128]{1,0:T(8,128)(2,1)}, bf16[992,128]{1,0:T(8,128)(2,1)S(1)}, u32[]{:S(2)}, u32[]{:S(2)}) collective-permute-start(bf16[992,128]{1,0:T(8,128)(2,1)} %get-tuple-element.397), channel_id=1, source_target_pairs={{0,62},{2,0},{4,2},{6,4},{8,6},{10,8},{12,10},{14,12},{16,14},{18,... | collective-permute-start | bytes 761864 | tf_op jit(solution)/shard_map/ppermute | solution.py:247
  (243 other events, 1351.8 us)

commit v2 on v0

v2 whole, which is shorter than its diff:
```python
import jax
import jax.numpy as jnp
from jax import lax
from jax.experimental import pallas as pl
from jax.experimental.pallas import tpu as pltpu
from jax.sharding import Mesh
from jax.sharding import PartitionSpec as P

HEADS = 32
KVH = 16
HD = 128
SHARED = HEADS // KVH
WIDE = SHARED * HD
CORES = 2
RING, CORE = "tp_0", "tp_1"

query_scale = 144.0 ** (-0.5)
soft_cap = 50.0
tanh_scale = query_scale / soft_cap
exp_scale = soft_cap * 1.4426950408889634

TILE = 1024
SPAN = 256
UNROLL = 2
PART = 256


def vmem():
    return pl.BlockSpec(memory_space=pltpu.VMEM)


def smem():
    return pl.BlockSpec(memory_space=pltpu.SMEM)


def pack(queries, keys, values):
    seqs, rows, _ = queries.shape

    def body(q_ref, k_ref, v_ref, out):
        for seq in range(seqs):
            for head in range(KVH):
                at = (seq * KVH + head) * rows
                out[at : at + rows, :WIDE] = q_ref[seq, :, head * WIDE : (head + 1) * WIDE]
                out[at : at + rows, WIDE : WIDE + HD] = k_ref[seq, :, head * HD : (head + 1) * HD]
                out[at : at + rows, WIDE + HD :] = v_ref[seq, :, head * HD : (head + 1) * HD]

    return pl.pallas_call(
        body,
        grid=(1,),
        out_shape=jax.ShapeDtypeStruct((seqs * KVH * rows, WIDE + 2 * HD), queries.dtype),
        in_specs=[vmem()] * 3,
        out_specs=vmem(),
        name="pack",
    )(queries, keys, values)


def attend(mine, other, place, rows):
    length = mine.shape[0]
    tiles = length // TILE

    def body(place_ref, x_ref, y_ref, out):
        core = place_ref[0]
        valid = place_ref[1]

        def weights(q, ref, at, lane, size):
            k = ref[pl.ds(at, size), lane : lane + HD]
            score = lax.dot_general(q, k, (((1,), (1,)), ((), ())), preferred_element_type=jnp.float32)
            return jnp.exp2(jnp.tanh(score * tanh_scale) * exp_scale)

        def mix(weight, ref, at, lane, size):
            v = ref[pl.ds(at, size), lane : lane + HD]
            return lax.dot_general(
                weight.astype(jnp.bfloat16), v, (((1,), (0,)), ((), ())), preferred_element_type=jnp.float32
            )

        def by_lane(weight):
            total = weight[:, :HD]
            for at in range(HD, weight.shape[1], HD):
                total = total + weight[:, at : at + HD]
            return total

        sources = ((x_ref, WIDE), (y_ref, 0))

        def one_tile(index, carry):
            first = pl.multiple_of(index * TILE, TILE)

            @pl.when(first * CORES < valid)
            def _():
                qs = [x_ref[pl.ds(first, TILE), h * HD : (h + 1) * HD] for h in range(SHARED)]

                def step(j, state):
                    state = [list(s) for s in state]
                    for u in range(UNROLL):
                        at = pl.multiple_of((j * UNROLL + u) * SPAN, SPAN)
                        for ref, lane in sources:
                            for h in range(SHARED):
                                weight = weights(qs[h], ref, at, lane, SPAN)
                                state[h][0] = state[h][0] + mix(weight, ref, at, lane + HD, SPAN)
                                state[h][1] = state[h][1] + by_lane(weight)
                    return tuple(tuple(s) for s in state)

                zero = jnp.zeros((TILE, HD), jnp.float32)
                state = lax.fori_loop(0, index * (TILE // (SPAN * UNROLL)), step, ((zero, zero),) * SHARED)
                for at in range(0, TILE, PART):
                    row = lax.broadcasted_iota(jnp.int32, (PART, 1), 0) + at
                    token = (row // rows) * (rows * CORES) + core * rows + lax.rem(row, rows)
                    live = first * CORES + token < valid
                    limits = (row, (row // rows + core) * rows - 1)
                    size = at + PART
                    key = lax.broadcasted_iota(jnp.int32, (PART, size), 1)
                    for h in range(SHARED):
                        acc = state[h][0][at:size]
                        total = state[h][1][at:size]
                        for (ref, lane), limit in zip(sources, limits):
                            weight = weights(qs[h][at:size], ref, first, lane, size)
                            weight = jnp.where(key <= limit, weight, 0.0)
                            acc = acc + mix(weight, ref, first, lane + HD, size)
                            total = total + by_lane(weight)
                        result = acc / jnp.sum(total, axis=1, keepdims=True)
                        result = jnp.where(live, result, 0.0).astype(jnp.bfloat16)
                        out[pl.ds(pl.multiple_of(first + at, PART), PART), h * HD : (h + 1) * HD] = result

            @pl.when(first * CORES >= valid)
            def _():
                out[pl.ds(first, TILE), :] = jnp.zeros((TILE, WIDE), jnp.bfloat16)

            return carry

        lax.fori_loop(0, tiles, one_tile, 0)

    return pl.pallas_call(
        body,
        grid=(1,),
        out_shape=jax.ShapeDtypeStruct((length, WIDE), mine.dtype),
        in_specs=[smem(), vmem(), vmem()],
        out_specs=vmem(),
        name="attend",
    )(place, mine, other)


def per_device(queries, keys, values, lengths):
    seqs, rows, _ = queries.shape
    core = lax.axis_index(CORE)
    own_seq = lax.axis_index(RING) // KVH
    valid = jnp.sum(jnp.where(jnp.arange(seqs) == own_seq, lengths, 0))
    place = jnp.stack([core, valid]).astype(jnp.int32)
    blocks = pack(queries, keys, values)
    mine = lax.all_to_all(blocks, RING, 0, 0, tiled=True)
    other = lax.ppermute(mine[:, WIDE:], CORE, [(i, CORES - 1 - i) for i in range(CORES)])
    output = attend(mine, other, place, rows)
    back = lax.all_to_all(output, RING, 0, 0, tiled=True)
    return back.reshape(seqs, KVH, rows, WIDE).transpose(0, 2, 1, 3).reshape(seqs, rows, HEADS * HD)


def solution(mesh):
    groups = mesh.shape["groups"]
    torus = Mesh(mesh.devices.reshape(groups, -1, CORES), ("groups", RING, CORE))
    placed = P("groups", (RING, CORE), None)
    return jax.shard_map(
        per_device, mesh=torus, in_specs=(placed, placed, placed, P("groups")), out_specs=placed, check_vma=False
    )
```

time: 390 us -> 369 us (0.946); the launches traced: 383 us -> 366 us
  blocking collectives: 120 us -> 338 us
  waiting for transfers between devices: 189 us -> 0.94 us
  starting transfers between devices: 31.6 us -> 0.01 us
  matrix products: 25.9 us -> 0 us
  Pallas kernels: 0 us -> 21.3 us
  other arithmetic: 9.96 us -> 1.92 us
    all_to_all x2, blocking collectives: 120 us -> 338 us  [the longest x1 225 us: per_device(): mine = lax.all_to_all(blocks, RING, 0, 0, tiled=True)]
    all_to_all x1 -> x0, waiting for transfers between devices: 189 us -> none  [sent_together(): lax.all_to_all(both, axis, split_axis=split_dim, concat_axis=concat_dim,...]
    all_to_all x1 -> x0, starting transfers between devices: 31.6 us -> none  [sent_together(): lax.all_to_all(both, axis, split_axis=split_dim, concat_axis=concat_dim,...]
    dot_general x16 -> x0, matrix products: 25.9 us -> none  [the longest x8 19.2 us: block_attend(): jnp.einsum('gqd,gkd->gqk', block_q, key_rows, preferred_element_type=jnp....]
    pallas_call x0 -> x2, Pallas kernels: none -> 21.3 us  [the longest x1 18.2 us: attend(): pl.pallas_call(body, grid=(1,), out_shape=jax.ShapeDtypeStruct((length, W...]
    lt x12 -> x0, other arithmetic: 7.34 us -> none  [the longest x7 4.28 us: block_attend(): key_pos[None, None, :] < valid[:, None, None]]
  transfers between devices with their start and end apart: 2 -> 1, of which waited for: 1 -> 1; matrix products, arithmetic and copies ran while one was open for 2% -> 1% of each run, Pallas kernels for 0% -> 0%
where the time goes in v2:
time: 369 us; the launch traced here: 366 us
  blocking collectives  338 us (92%)
  Pallas kernels  21.3 us (6%)
  local copies, waits for them, and re-layouts  3.98 us (1%)
    all_to_all x1, blocking collectives, per_device(): mine = lax.all_to_all(blocks, RING, 0, 0, tiled=True)  225 us
    all_to_all x1, blocking collectives, per_device(): back = lax.all_to_all(output, RING, 0, 0, tiled=True)  113 us
    pallas_call x1, Pallas kernels, attend(): pl.pallas_call(body, grid=(1,), out_shape=jax.ShapeDtypeStruct((length, W...  18.2 us
  transfers between devices with their start and end apart: 1, of which 1 were waited for; matrix products, arithmetic and copies ran while one was open for 1% of the time, Pallas kernels for 0%

profile of v2, /device:TPU:228, one launch (start us, length us, event | category | flops | bytes accessed | tf_op | source)
XLA Modules:
  0.0 366.0 jit_solution(14244877517327511580)
XLA Ops:
  0.0 3.1 pack.1
  3.1 224.7 %all_to_all.20 = bf16[32,64,512]{2,1,0:T(8,128)(2,1)S(1)} all-to-all(bf16[32,64,512]{2,1,0:T(8,128)(2,1)} %bitcast.13), channel_id=1, replica_groups=mesh['groups'=4,'tp_0'=32,'tp_1'=2] {'tp_0'}, dimensions={0} | all-to-all | bytes 4194304 | tf_op jit(solution)/shard_map/all_to_all | solution.py:148
  227.8 0.0 copy-start
  227.8 0.0 copy-start.2
  227.8 1.1 slice.4
  228.9 0.0 collective-permute-start
  228.9 0.0 copy-done.2
  228.9 0.6 fusion
  229.6 1.3 pad_add_fusion.place_ref
  230.9 0.9 collective-permute-done.y_ref
  231.8 0.0 copy-done
  231.8 0.0 copy-start.1
  231.8 1.0 copy-done.1
  232.8 18.2 %attend.1 = bf16[2048,256]{1,0:T(8,128)(2,1)} custom-call(s32[2]{0:T(128)} %pad_add_fusion.place_ref, bf16[2048,512]{1,0:T(8,128)(2,1)} %bitcast.12, bf16[2048,256]{1,0:T(8,128)(2,1)} %copy-done.1), custom_call_target="tpu_custom_call" | custom-call | tf_op jit(solution)/shard_map/attend/pallas_call | solution.py:131
  251.0 113.1 %all_to_all.21 = bf16[32,64,256]{2,1,0:T(8,128)(2,1)S(1)} all-to-all(bf16[32,64,256]{2,1,0:T(8,128)(2,1)} %bitcast.14), channel_id=1, replica_groups=mesh['groups'=4,'tp_0'=32,'tp_1'=2] {'tp_0'}, dimensions={0} | all-to-all | bytes 2097152 | tf_op jit(solution)/shard_map/all_to_all | solution.py:151
  364.1 0.6 copy.7
  364.7 1.3 reshape.12
Async XLA Ops:
  227.8 4.0 %copy-start = (bf16[32,64,512]{2,1,0:T(8,128)(2,1)}, bf16[32,64,512]{2,1,0:T(8,128)(2,1)S(1)}, u32[]{:S(2)}) copy-start(bf16[32,64,512]{2,1,0:T(8,128)(2,1)S(1)} %all_to_all.20) | copy-start | bytes 6291460
  227.8 1.1 copy-start.2
  228.9 2.9 collective-permute-start
  231.8 1.0 copy-start.1

commit v3 on v2

--- a/solution.py
+++ b/solution.py
@@ -23,6 +23,8 @@
 SPAN = 256
 UNROLL = 2
 PART = 256
+STEPS = 2
+ROOM = 40 * 1024 * 1024
 
 
 def vmem():
@@ -35,23 +37,44 @@
 
 def pack(queries, keys, values):
     seqs, rows, _ = queries.shape
+    few = KVH // STEPS
 
     def body(q_ref, k_ref, v_ref, out):
-        for seq in range(seqs):
-            for head in range(KVH):
-                at = (seq * KVH + head) * rows
-                out[at : at + rows, :WIDE] = q_ref[seq, :, head * WIDE : (head + 1) * WIDE]
-                out[at : at + rows, WIDE : WIDE + HD] = k_ref[seq, :, head * HD : (head + 1) * HD]
-                out[at : at + rows, WIDE + HD :] = v_ref[seq, :, head * HD : (head + 1) * HD]
+        for head in range(few):
+            at = head * rows
+            out[at : at + rows, :WIDE] = q_ref[0, :, head * WIDE : (head + 1) * WIDE]
+            out[at : at + rows, WIDE : WIDE + HD] = k_ref[0, :, head * HD : (head + 1) * HD]
+            out[at : at + rows, WIDE + HD :] = v_ref[0, :, head * HD : (head + 1) * HD]
+
+    def cut(width):
+        return pl.BlockSpec((1, rows, few * width), lambda s, i: (s, 0, i))
 
     return pl.pallas_call(
         body,
-        grid=(1,),
+        grid=(seqs, STEPS),
         out_shape=jax.ShapeDtypeStruct((seqs * KVH * rows, WIDE + 2 * HD), queries.dtype),
-        in_specs=[vmem()] * 3,
-        out_specs=vmem(),
+        in_specs=[cut(WIDE), cut(HD), cut(HD)],
+        out_specs=pl.BlockSpec((few * rows, WIDE + 2 * HD), lambda s, i: (s * STEPS + i, 0)),
         name="pack",
     )(queries, keys, values)
+
+
+def unpack(blocks, seqs, rows):
+    few = KVH // STEPS
+
+    def body(x_ref, out):
+        for head in range(few):
+            out[0, :, head * WIDE : (head + 1) * WIDE] = x_ref[head * rows : (head + 1) * rows, :]
+
+    return pl.pallas_call(
+        body,
+        grid=(seqs, STEPS),
+        out_shape=jax.ShapeDtypeStruct((seqs, rows, KVH * WIDE), blocks.dtype),
+        in_specs=[pl.BlockSpec((few * rows, WIDE), lambda s, i: (s * STEPS + i, 0))],
+        out_specs=pl.BlockSpec((1, rows, few * WIDE), lambda s, i: (s, 0, i)),
+        compiler_params=pltpu.CompilerParams(vmem_limit_bytes=ROOM),
+        name="unpack",
+    )(blocks)
 
 
 def attend(mine, other, place, rows):
@@ -130,10 +153,10 @@
 
     return pl.pallas_call(
         body,
-        grid=(1,),
         out_shape=jax.ShapeDtypeStruct((length, WIDE), mine.dtype),
         in_specs=[smem(), vmem(), vmem()],
         out_specs=vmem(),
+        compiler_params=pltpu.CompilerParams(vmem_limit_bytes=ROOM),
         name="attend",
     )(place, mine, other)
 
@@ -149,7 +172,7 @@
     other = lax.ppermute(mine[:, WIDE:], CORE, [(i, CORES - 1 - i) for i in range(CORES)])
     output = attend(mine, other, place, rows)
     back = lax.all_to_all(output, RING, 0, 0, tiled=True)
-    return back.reshape(seqs, KVH, rows, WIDE).transpose(0, 2, 1, 3).reshape(seqs, rows, HEADS * HD)
+    return unpack(back, seqs, rows)
 
 
 def solution(mesh):

time: 369 us -> 365 us (0.989)
    pallas_call x2 -> x3, Pallas kernels: 21.3 us -> 21.2 us  [the longest x1 15.9 us: attend(): pl.pallas_call(body, out_shape=jax.ShapeDtypeStruct((length, WIDE), mine....]
  transfers between devices with their start and end apart: 1 -> 1, of which waited for: 1 -> 1; matrix products, arithmetic and copies ran while one was open for 1% -> 0% of each run, Pallas kernels for 0% -> 0%
where the time goes in v3:
time: 365 us; the launch traced here: 363 us
  blocking collectives  338 us (93%)
  Pallas kernels  21.2 us (6%)
    all_to_all x1, blocking collectives, per_device(): mine = lax.all_to_all(blocks, RING, 0, 0, tiled=True)  225 us
    all_to_all x1, blocking collectives, per_device(): back = lax.all_to_all(output, RING, 0, 0, tiled=True)  113 us
    pallas_call x1, Pallas kernels, attend(): pl.pallas_call(body, out_shape=jax.ShapeDtypeStruct((length, WIDE), mine....  15.9 us
  transfers between devices with their start and end apart: 1, of which 1 were waited for; matrix products, arithmetic and copies ran while one was open for 0% of the time, Pallas kernels for 0%

profile of v3, /device:TPU:228, one launch (start us, length us, event | category | flops | bytes accessed | tf_op | source)
XLA Modules:
  0.0 362.8 jit_solution(16820123113269289530)
XLA Ops:
  0.0 3.8 %pack.1 = bf16[2048,512]{1,0:T(8,128)(2,1)} custom-call(bf16[2,64,4096]{2,1,0:T(8,128)(2,1)} %q_ref.1, bf16[2,64,2048]{2,1,0:T(8,128)(2,1)} %k_ref.1, bf16[2,64,2048]{2,1,0:T(8,128)(2,1)} %v_ref.1), custom_call_target="tpu_custom_call" | custom-call | tf_op jit(solution)/shard_map/pack/pallas_call | solution.py:52
  3.8 224.7 %all_to_all.22 = bf16[32,64,512]{2,1,0:T(8,128)(2,1)S(1)} all-to-all(bf16[32,64,512]{2,1,0:T(8,128)(2,1)} %bitcast.10), channel_id=1, replica_groups=mesh['groups'=4,'tp_0'=32,'tp_1'=2] {'tp_0'}, dimensions={0} | all-to-all | bytes 4194304 | tf_op jit(solution)/shard_map/all_to_all | solution.py:171
  228.6 0.0 copy-start
  228.6 1.0 slice.4
  229.6 0.0 collective-permute-start
  229.6 0.0 copy-done
  229.6 0.7 fusion
  230.3 0.8 pad_add_fusion.place_ref
  231.1 1.4 collective-permute-done.y_ref
  232.5 15.9 %attend.1 = bf16[2048,256]{1,0:T(8,128)(2,1)S(1)} custom-call(s32[2]{0:T(128)S(1)} %pad_add_fusion.place_ref, bf16[2048,512]{1,0:T(8,128)(2,1)S(1)} %bitcast.7, bf16[2048,256]{1,0:T(8,128)(2,1)S(1)} %collective-permute-done.y_ref), custom_call_target="tpu_custom_call" | custom-call | tf_op jit(solution)/shard_map/attend/pallas_call | solution.py:154
  248.4 112.9 %all_to_all.23 = bf16[32,64,256]{2,1,0:T(8,128)(2,1)S(1)} all-to-all(bf16[32,64,256]{2,1,0:T(8,128)(2,1)S(1)} %bitcast.8), channel_id=1, replica_groups=mesh['groups'=4,'tp_0'=32,'tp_1'=2] {'tp_0'}, dimensions={0} | all-to-all | bytes 2097152 | tf_op jit(solution)/shard_map/all_to_all | solution.py:174
  361.3 1.5 unpack.1
Async XLA Ops:
  228.6 1.0 copy-start
  229.6 2.9 collective-permute-start

commit v4 on v3

--- a/solution.py
+++ b/solution.py
@@ -21,7 +21,7 @@
 
 TILE = 1024
 SPAN = 256
-UNROLL = 2
+UNROLL = 4
 PART = 256
 STEPS = 2
 ROOM = 40 * 1024 * 1024
@@ -37,24 +37,21 @@
 
 def pack(queries, keys, values):
     seqs, rows, _ = queries.shape
-    few = KVH // STEPS
 
     def body(q_ref, k_ref, v_ref, out):
-        for head in range(few):
-            at = head * rows
-            out[at : at + rows, :WIDE] = q_ref[0, :, head * WIDE : (head + 1) * WIDE]
-            out[at : at + rows, WIDE : WIDE + HD] = k_ref[0, :, head * HD : (head + 1) * HD]
-            out[at : at + rows, WIDE + HD :] = v_ref[0, :, head * HD : (head + 1) * HD]
-
-    def cut(width):
-        return pl.BlockSpec((1, rows, few * width), lambda s, i: (s, 0, i))
+        for seq in range(seqs):
+            for head in range(KVH):
+                at = (seq * KVH + head) * rows
+                out[at : at + rows, :WIDE] = q_ref[seq, :, head * WIDE : (head + 1) * WIDE]
+                out[at : at + rows, WIDE : WIDE + HD] = k_ref[seq, :, head * HD : (head + 1) * HD]
+                out[at : at + rows, WIDE + HD :] = v_ref[seq, :, head * HD : (head + 1) * HD]
 
     return pl.pallas_call(
         body,
-        grid=(seqs, STEPS),
+        grid=(1,),
         out_shape=jax.ShapeDtypeStruct((seqs * KVH * rows, WIDE + 2 * HD), queries.dtype),
-        in_specs=[cut(WIDE), cut(HD), cut(HD)],
-        out_specs=pl.BlockSpec((few * rows, WIDE + 2 * HD), lambda s, i: (s * STEPS + i, 0)),
+        in_specs=[vmem()] * 3,
+        out_specs=vmem(),
         name="pack",
     )(queries, keys, values)
 

time: 365 us -> 364 us (level)
  no operation moved by 1% of the time
where the time goes in v4:
time: 364 us; the launch traced here: 362 us
  blocking collectives  338 us (93%)
  Pallas kernels  20 us (5%)
    all_to_all x1, blocking collectives, per_device(): mine = lax.all_to_all(blocks, RING, 0, 0, tiled=True)  225 us
    all_to_all x1, blocking collectives, per_device(): back = lax.all_to_all(output, RING, 0, 0, tiled=True)  113 us
    pallas_call x1, Pallas kernels, attend(): pl.pallas_call(body, out_shape=jax.ShapeDtypeStruct((length, WIDE), mine....  15.4 us
  transfers between devices with their start and end apart: 1, of which 1 were waited for; matrix products, arithmetic and copies ran while one was open for 0% of the time, Pallas kernels for 0%

profile of v4, /device:TPU:228, one launch (start us, length us, event | category | flops | bytes accessed | tf_op | source)
XLA Modules:
  0.0 361.6 jit_solution(16408518393288765146)
XLA Ops:
  0.0 3.1 pack.1
  3.1 224.7 %all_to_all.22 = bf16[32,64,512]{2,1,0:T(8,128)(2,1)S(1)} all-to-all(bf16[32,64,512]{2,1,0:T(8,128)(2,1)} %bitcast.10), channel_id=1, replica_groups=mesh['groups'=4,'tp_0'=32,'tp_1'=2] {'tp_0'}, dimensions={0} | all-to-all | bytes 4194304 | tf_op jit(solution)/shard_map/all_to_all | solution.py:168
  227.8 0.0 copy-start
  227.8 1.0 slice.4
  228.9 0.0 collective-permute-start
  228.9 0.0 copy-done
  228.9 0.7 fusion
  229.6 0.8 pad_add_fusion.place_ref
  230.4 1.4 collective-permute-done.y_ref
  231.8 15.4 %attend.1 = bf16[2048,256]{1,0:T(8,128)(2,1)S(1)} custom-call(s32[2]{0:T(128)S(1)} %pad_add_fusion.place_ref, bf16[2048,512]{1,0:T(8,128)(2,1)S(1)} %bitcast.7, bf16[2048,256]{1,0:T(8,128)(2,1)S(1)} %collective-permute-done.y_ref), custom_call_target="tpu_custom_call" | custom-call | tf_op jit(solution)/shard_map/attend/pallas_call | solution.py:151
  247.1 112.9 %all_to_all.23 = bf16[32,64,256]{2,1,0:T(8,128)(2,1)S(1)} all-to-all(bf16[32,64,256]{2,1,0:T(8,128)(2,1)S(1)} %bitcast.8), channel_id=1, replica_groups=mesh['groups'=4,'tp_0'=32,'tp_1'=2] {'tp_0'}, dimensions={0} | all-to-all | bytes 2097152 | tf_op jit(solution)/shard_map/all_to_all | solution.py:171
  360.1 1.5 unpack.1
Async XLA Ops:
  227.8 1.0 copy-start
  228.9 2.9 collective-permute-start

commit v5 on v4

--- a/solution.py
+++ b/solution.py
@@ -20,8 +20,8 @@
 exp_scale = soft_cap * 1.4426950408889634
 
 TILE = 1024
-SPAN = 256
-UNROLL = 4
+SPAN = 512
+UNROLL = 2
 PART = 256
 STEPS = 2
 ROOM = 40 * 1024 * 1024

time: 364 us -> 365 us (level)
  no operation moved by 1% of the time
where the time goes in v5:
time: 365 us; the launch traced here: 362 us
  blocking collectives  338 us (93%)
  Pallas kernels  20 us (5%)
    all_to_all x1, blocking collectives, per_device(): mine = lax.all_to_all(blocks, RING, 0, 0, tiled=True)  225 us
    all_to_all x1, blocking collectives, per_device(): back = lax.all_to_all(output, RING, 0, 0, tiled=True)  113 us
    pallas_call x1, Pallas kernels, attend(): pl.pallas_call(body, out_shape=jax.ShapeDtypeStruct((length, WIDE), mine....  15.4 us
  transfers between devices with their start and end apart: 1, of which 1 were waited for; matrix products, arithmetic and copies ran while one was open for 0% of the time, Pallas kernels for 0%

profile of v5, /device:TPU:228, one launch (start us, length us, event | category | flops | bytes accessed | tf_op | source)
XLA Modules:
  0.0 361.6 jit_solution(3867878205448978749)
XLA Ops:
  0.0 3.1 pack.1
  3.1 224.7 %all_to_all.22 = bf16[32,64,512]{2,1,0:T(8,128)(2,1)S(1)} all-to-all(bf16[32,64,512]{2,1,0:T(8,128)(2,1)} %bitcast.10), channel_id=1, replica_groups=mesh['groups'=4,'tp_0'=32,'tp_1'=2] {'tp_0'}, dimensions={0} | all-to-all | bytes 4194304 | tf_op jit(solution)/shard_map/all_to_all | solution.py:168
  227.8 0.0 copy-start
  227.8 1.0 slice.4
  228.9 0.0 collective-permute-start
  228.9 0.0 copy-done
  228.9 0.7 fusion
  229.6 0.8 pad_add_fusion.place_ref
  230.4 1.4 collective-permute-done.y_ref
  231.8 15.4 %attend.1 = bf16[2048,256]{1,0:T(8,128)(2,1)S(1)} custom-call(s32[2]{0:T(128)S(1)} %pad_add_fusion.place_ref, bf16[2048,512]{1,0:T(8,128)(2,1)S(1)} %bitcast.7, bf16[2048,256]{1,0:T(8,128)(2,1)S(1)} %collective-permute-done.y_ref), custom_call_target="tpu_custom_call" | custom-call | tf_op jit(solution)/shard_map/attend/pallas_call | solution.py:151
  247.1 112.9 %all_to_all.23 = bf16[32,64,256]{2,1,0:T(8,128)(2,1)S(1)} all-to-all(bf16[32,64,256]{2,1,0:T(8,128)(2,1)S(1)} %bitcast.8), channel_id=1, replica_groups=mesh['groups'=4,'tp_0'=32,'tp_1'=2] {'tp_0'}, dimensions={0} | all-to-all | bytes 2097152 | tf_op jit(solution)/shard_map/all_to_all | solution.py:171
  360.1 1.5 unpack.1
Async XLA Ops:
  227.8 1.0 copy-start
  228.9 2.9 collective-permute-start
